TPU v7x, 32 devices: a whole 2x2x4 slice. The times are simulated.
32 devices in a mesh: lat: 8 (over z, y), ch: 4 (over x, core).
Axes of the slice: x: 2, y: 2, z: 4, core: 2. Of those that a mesh axis runs over, the one named last changes fastest.
Arguments:
- field: bfloat16 [728, 256, 1440], P('lat', 'ch'), may hold values from -6 to 6
- legendre: bfloat16 [384, 721, 728], P(('lat', 'ch')), may hold values from -0.21875 to 0.21875
- pair_order: int32 [384], replicated, may hold values from 0 to 383, each once
Outputs:
- coeffs: float32 [384, 721, 2, 256], P(('lat', 'ch'))
Inputs may be any that keep to these rules, and one draw needn't show every extreme that they name: `pair_order`: each of 0 to 383 appears once; a value p below 360 gives its bin the orders p and 719 - p, and a bin with a larger value is empty.
All inputs are finite; a program needn't handle non-finite values.
Results may differ from a plain program's by a relative error of at most 0.0037.
Values may be sent and summed in bfloat16 or wider, within the bound.
A program may use at most 256 MiB of HBM per device.

v0:
```python
import math

import jax
import jax.numpy as jnp
from jax import lax
from jax.sharding import PartitionSpec as P

NLAT = 721


def dft_table(points, modes, lon_count):
    turns = points[:, None] * modes[None, :] % lon_count
    angle = turns.astype(jnp.float32) * (2.0 * math.pi / lon_count)
    return jnp.stack([jnp.cos(angle), -jnp.sin(angle)], axis=-1).astype(jnp.bfloat16)


def project(basis_piece, data_rows, boundary, keep_mask):
    products = jnp.einsum(
        "brl,lbn->brn", basis_piece, data_rows, preferred_element_type=jnp.float32
    )
    bin_count, row_count, width_all = products.shape
    products = products.reshape(bin_count, row_count, 2, 2, width_all // 4)
    degree = jnp.arange(row_count, dtype=jnp.int32)
    upper_part = degree[None, :, None, None] < boundary[:, None, None, None]
    chosen = jnp.where(upper_part, products[:, :, 0], products[:, :, 1])
    return chosen * keep_mask[:, None, None, None].astype(jnp.float32)


def per_device(field, legendre, pair_order):
    lat_rows, chan_dev, lon_count = field.shape
    slot_count = pair_order.shape[0]
    lat_count = lax.axis_size("lat")
    group_size = slot_count // lat_count
    max_order = legendre.shape[1] - 1
    keep_all = pair_order < max_order // 2
    first_order = jnp.where(keep_all, pair_order, 0)
    orders = jnp.stack([first_order, max_order - 1 - first_order], axis=1)
    bound_all = max_order - first_order
    rows_global = lax.axis_index("lat") * lat_rows + jnp.arange(lat_rows, dtype=jnp.int32)
    masked = jnp.where((rows_global < NLAT)[:, None, None], field, jnp.zeros_like(field))
    norm_scale = 2.0 * math.pi / lon_count
    points = jnp.arange(lon_count, dtype=jnp.int32)
    dft_basis = dft_table(points, orders.reshape(-1), lon_count).reshape(lon_count, 4 * slot_count)
    fourier = jnp.einsum("ack,kn->anc", masked, dft_basis, preferred_element_type=jnp.float32)
    fourier = (fourier * norm_scale).astype(jnp.bfloat16).reshape(lat_rows, slot_count, 4, chan_dev)
    received = lax.all_to_all(
        fourier.reshape(lat_rows, slot_count, 4 * chan_dev),
        "lat",
        split_axis=1,
        concat_axis=0,
        tiled=True,
    )
    group_start = lax.axis_index("lat") * group_size
    bound_group = lax.dynamic_slice_in_dim(bound_all, group_start, group_size)
    keep_group = lax.dynamic_slice_in_dim(keep_all, group_start, group_size)
    part_sums = project(
        lax.all_gather(legendre, "ch", axis=0, tiled=True), received, bound_group, keep_group
    )
    return lax.all_to_all(part_sums, "ch", split_axis=0, concat_axis=3, tiled=True)


def solution(mesh):
    in_specs = (P("lat", "ch", None), P(("lat", "ch"), None, None), P())
    out_specs = P(("lat", "ch"), None, None, None)
    return jax.shard_map(
        per_device, mesh=mesh, in_specs=in_specs, out_specs=out_specs, check_vma=False
    )
```

profile of v0, /device:TPU:0, one launch (start us, length us, event | category | flops | bytes accessed | tf_op | source)
XLA Modules:
  0.0 950.9 jit_solution(16822089257262218695)
XLA Ops:
  6.5 0.7 all-gather.2.cloned.1.call-update
  7.3 0.7 broadcast_subtract_fusion.1
  8.0 0.1 copy.30
  8.1 0.1 mul.66
  8.3 19.0 %cosine_convert_fusion = (bf16[1440,768,1]{1,0,2:T(8,128)(2,1)S(1)}, bf16[1440,768,1]{1,0,2:T(8,128)(2,1)S(1)}) fusion(s32[768]{0:T(1024)S(1)} %mul.66), kind=kLoop, calls=%fused_computation.18 | loop fusion | flops 13271040 | bytes 4426752 | tf_op jit(solution)/shard_map/convert
  27.3 3.2 pad_maximum_fusion
  30.6 13.2 %copy.31 = bf16[1440,768,2]{0,2,1:T(2,128)(2,1)} copy(bf16[1440,768,2]{1,0,2:T(8,128)(2,1)} %pad_maximum_fusion) | data formatting | bytes 8847360 | tf_op jit(solution)/shard_map/stack | solution.py:14
  43.8 10.9 %convert_element_type.30 = bf16[1440,1536]{0,1:T(8,128)(2,1)} reshape(bf16[1440,768,2]{0,2,1:T(2,128)(2,1)} %copy.31) | data formatting | bytes 8847360 | tf_op jit(solution)/shard_map/convert_element_type | solution.py:14
  54.7 16.6 %broadcast_select_fusion = bf16[91,64,1440]{2,1,0:T(8,128)(2,1)} fusion(bf16[91,64,1440]{2,1,0:T(8,128)(2,1)} %param.3, pred[91]{0:T(512)(128)(4,1)S(1)} %add_compare_fusion), kind=kLoop, calls=%fused_computation.10 | loop fusion | flops 8386560 | bytes 33546332 | tf_op jit(solution)/shard_map/jit(_where)/select_n | solution.py:40
  71.3 49.8 %fusion = bf16[91,1536,64]{1,0,2:T(8,128)(2,1)} fusion(bf16[91,64,1440]{2,1,0:T(8,128)(2,1)} %broadcast_select_fusion, bf16[1440,1536]{0,1:T(8,128)(2,1)S(1)} %copy-done), kind=kOutput, calls=%fused_computation.1 | convolution fusion | flops 25781403648 | bytes 39088128 | tf_op jit(solution)/shard_map/ack,kn->anc/dot_general | solution.py:44
  121.2 31.3 %copy.34 = bf16[91,1536,64]{0,2,1:T(8,128)(2,1)} copy(bf16[91,1536,64]{1,0,2:T(8,128)(2,1)} %fusion) | data formatting | bytes 35782656 | tf_op jit(solution)/shard_map/convert_element_type | solution.py:45
  152.5 28.4 %copy.35 = bf16[91,384,256]{2,0,1:T(8,128)(2,1)} copy(bf16[91,384,256]{0,2,1:T(8,128)(2,1)} %bitcast.33) | data formatting | bytes 35782656 | tf_op jit(solution)/shard_map/reshape;reshape | solution.py:47
  180.9 7.3 all-to-all-start
  188.1 0.1 dynamic_slice.6
  188.2 0.1 dynamic-slice_convert_fusion
  188.3 0.1 iota_compare_fusion
  188.4 408.6 %all-to-all-done = bf16[91,384,256]{2,0,1:T(8,128)(2,1)} async-done(((bf16[91,384,256]{2,0,1:T(8,128)(2,1)}), bf16[91,384,256]{2,0,1:T(8,128)(2,1)}, u32[]{:S(2)}, u32[]{:S(2)}) %all-to-all-start) | async-done | bytes 17891360 | tf_op jit(solution)/shard_map/all_to_all | solution.py:46
  596.9 19.0 %copy.37 = bf16[8,91,48,256]{3,2,1,0:T(8,128)(2,1)} copy(bf16[8,91,48,256]{3,1,2,0:T(8,128)(2,1)} %bitcast.5) | data formatting | bytes 35782656 | tf_op jit(solution)/shard_map/all_to_all | solution.py:46
  615.9 36.0 %fusion.9 = f32[48,721,256]{2,1,0:T(8,128)} fusion(bf16[48,721,728]{2,1,0:T(8,128)(2,1)} %all-gather.2.cloned.1.call-done, bf16[728,48,256]{2,1,0:T(8,128)(2,1)} %bitcast.36), kind=kOutput, calls=%fused_computation.11 | convolution fusion | flops 12899647488 | bytes 103719168 | tf_op jit(solution)/shard_map/brl,lbn->brn/dot_general | solution.py:18
  651.9 36.0 %copy.39 = f32[48,721,256]{1,2,0:T(8,128)} copy(f32[48,721,256]{2,1,0:T(8,128)} %fusion.9) | data formatting | bytes 70877184 | tf_op jit(solution)/shard_map/brl,lbn->brn/dot_general | solution.py:18
  687.9 12.8 %fusion.2 = f32[48,721,2,64]{1,3,2,0:T(8,128)S(1)} fusion(f32[48,721,2,2,64]{1,4,3,2,0:T(8,128)} %bitcast.32, f32[48]{0:T(128)S(1)} %dynamic-slice_convert_fusion, pred[48,721]{1,0:T(8,128)(4,1)S(1)} %iota_compare_fusion), kind=kLoop, calls=%fused_computation.4 | loop fusion | flops 8859648 | bytes 53192688 | tf_op jit(solution)/shard_map/mul | solution.py:26
  700.8 208.6 %all_to_all.36 = f32[48,721,2,64]{1,3,2,0:T(8,128)S(1)} all-to-all(f32[48,721,2,64]{1,3,2,0:T(8,128)S(1)} %fusion.2), channel_id=1, replica_groups=mesh['lat'=8,'ch'=4] {'ch'}, dimensions={0} | all-to-all | bytes 35438592 | tf_op jit(solution)/shard_map/all_to_all | solution.py:59
  909.4 6.9 copy.41
  916.4 27.7 %copy.42 = f32[12,721,2,256]{3,2,1,0:T(2,128)} copy(f32[12,721,2,256]{1,3,2,0:T(8,128)} %bitcast.35) | data formatting | bytes 35438592 | tf_op jit(solution)/shard_map/all_to_all | solution.py:59
  (11 shorter events, 0.0 us)
Async XLA Ops:
  6.5 609.4 %all-gather.2.cloned.1.call-start = ((), (), s32[]{:S(2)}) async-start(), calls=%async_computation.2 | async-start | bytes 67092480 | tf_op jit(solution)/shard_map/all_gather | solution.py:57
  54.7 16.6 %copy-start = (bf16[1440,1536]{0,1:T(8,128)(2,1)S(1)}, bf16[1440,1536]{0,1:T(8,128)(2,1)}, u32[]{:S(2)}) copy-start(bf16[1440,1536]{0,1:T(8,128)(2,1)} %convert_element_type.30) | copy-start | bytes 13271044
  180.9 7.3 copy-start.1
  180.9 416.1 %all-to-all-start = ((bf16[91,384,256]{2,0,1:T(8,128)(2,1)}), bf16[91,384,256]{2,0,1:T(8,128)(2,1)}, u32[]{:S(2)}, u32[]{:S(2)}) async-start(bf16[91,384,256]{2,0,1:T(8,128)(2,1)} %copy.35), calls=%async_computation | async-start | bytes 37748736 | tf_op jit(solution)/shard_map/all_to_all | solution.py:46
Sparse Core Ops, SparseCore 0:
  8.9 320.7 all-gather.1
where the time goes:
time: 955 us; the launch traced here: 951 us
  waiting for transfers between devices  409 us (43%)
  blocking collectives  209 us (22%)
  local copies, waits for them, and re-layouts  174 us (18%)
  matrix products  85.8 us (9%)
  other arithmetic  52.6 us (6%)
  between operations  13.4 us (1%)
    all_to_all x1, waiting for transfers between devices, per_device(): lax.all_to_all(fourier.reshape(lat_rows, slot_count, 4 * chan_dev), 'lat'...  409 us
    all_to_all x1, blocking collectives, per_device(): lax.all_to_all(part_sums, 'ch', split_axis=0, concat_axis=3, tiled=True)  209 us
    dot_general x1, matrix products, per_device(): jnp.einsum('ack,kn->anc', masked, dft_basis, preferred_element_type=jnp.f...  49.8 us
    dot_general x1, local copies, waits for them, and re-layouts, project(): jnp.einsum('brl,lbn->brn', basis_piece, data_rows, preferred_element_type...  36 us
    dot_general x1, matrix products, project(): jnp.einsum('brl,lbn->brn', basis_piece, data_rows, preferred_element_type...  36 us
    all_to_all x2, local copies, waits for them, and re-layouts, per_device(): lax.all_to_all(part_sums, 'ch', split_axis=0, concat_axis=3, tiled=True)  34.7 us
    convert_element_type x1, local copies, waits for them, and re-layouts, per_device(): (fourier * norm_scale).astype(jnp.bfloat16)  31.3 us
    another operation x1, local copies, waits for them, and re-layouts, per_device(): fourier.reshape(lat_rows, slot_count, 4 * chan_dev)  28.4 us
  transfers between devices with their start and end apart: 2, of which 1 were waited for; matrix products, arithmetic and copies ran while one was open for 20% of the time, Pallas kernels for 0%

commit v1 on v0

v1 whole, which is shorter than its diff:
```python
import math

import jax
import jax.numpy as jnp
from jax import lax
from jax.sharding import PartitionSpec as P

NLAT = 721
GROUPS = 4


def dft_table(points, modes, lon_count):
    columns = jnp.repeat(modes, 2)
    phase = jnp.tile(jnp.array([0, lon_count // 4], jnp.int32), modes.shape[0])
    turns = (points[:, None] * columns[None, :] + phase[None, :]) % lon_count
    angle = turns.astype(jnp.float32) * (2.0 * math.pi / lon_count)
    return jnp.cos(angle).astype(jnp.bfloat16)


def per_device(field, legendre, pair_order):
    lat_rows, chan_dev, lon_count = field.shape
    own, row_count, _ = legendre.shape
    lat_count = lax.axis_size("lat")
    ch_count = lax.axis_size("ch")
    dev_count = lat_count * ch_count
    me = lax.axis_index("lat") * ch_count + lax.axis_index("ch")
    max_order = row_count - 1
    keep_all = pair_order < max_order // 2
    first_order = jnp.where(keep_all, pair_order, 0)
    orders = jnp.stack([first_order, max_order - 1 - first_order], axis=1)
    bound_own = lax.dynamic_slice_in_dim(max_order - first_order, me * own, own)
    keep_own = lax.dynamic_slice_in_dim(keep_all, me * own, own)
    rows_global = lax.axis_index("lat") * lat_rows + jnp.arange(lat_rows, dtype=jnp.int32)
    in_grid = (rows_global < NLAT)[:, None, None]
    norm_scale = 2.0 * math.pi / lon_count
    points = jnp.arange(lon_count, dtype=jnp.int32)
    degree = jnp.arange(row_count, dtype=jnp.int32)
    groups = math.gcd(GROUPS, own)
    width = own // groups
    by_dev = orders.reshape(dev_count, own, 2)
    outs = []
    for g in range(groups):
        part = by_dev[:, g * width : (g + 1) * width].reshape(-1)
        basis = dft_table(points, part, lon_count)
        fourier = jnp.einsum("ack,kn->anc", field, basis, preferred_element_type=jnp.float32)
        fourier = jnp.where(in_grid, fourier * norm_scale, 0.0).astype(jnp.bfloat16)
        fourier = fourier.reshape(lat_rows, dev_count * width, 4 * chan_dev)
        got = lax.all_to_all(fourier, ("lat", "ch"), split_axis=1, concat_axis=0, tiled=True)
        got = got.reshape(lat_count, ch_count, lat_rows, width, 4, chan_dev)
        got = got.transpose(3, 0, 2, 4, 1, 5)
        got = got.reshape(width, lat_count * lat_rows, 4 * ch_count * chan_dev)
        products = jnp.einsum(
            "brl,bln->brn", legendre[g * width : (g + 1) * width], got, preferred_element_type=jnp.float32
        )
        bound = bound_own[g * width : (g + 1) * width]
        keep = keep_own[g * width : (g + 1) * width]
        upper = degree[None, :, None] < bound[:, None, None]
        half = products.shape[2] // 2
        chosen = jnp.where(upper, products[:, :, :half], products[:, :, half:])
        chosen = chosen * keep[:, None, None].astype(jnp.float32)
        outs.append(chosen.reshape(width, row_count, 2, half // 2))
    return outs[0] if groups == 1 else jnp.concatenate(outs, axis=0)


def solution(mesh):
    in_specs = (P("lat", "ch", None), P(("lat", "ch"), None, None), P())
    out_specs = P(("lat", "ch"), None, None, None)
    return jax.shard_map(
        per_device, mesh=mesh, in_specs=in_specs, out_specs=out_specs, check_vma=False
    )
```

time: 955 us -> 641 us (0.67)
  waiting for transfers between devices: 409 us -> 139 us
  blocking collectives: 209 us -> 0 us
  matrix products: 85.8 us -> 199 us
  local copies, waits for them, and re-layouts: 174 us -> 244 us
  other arithmetic: 52.6 us -> 27.2 us
  starting transfers between devices: 7.26 us -> 20.7 us
  between operations: 13.4 us -> 0.43 us
    all_to_all x1 -> x4, waiting for transfers between devices: 409 us -> 139 us  [per_device(): lax.all_to_all(fourier, ('lat', 'ch'), split_axis=1, concat_axis=0, tiled...]
    all_to_all x1 -> x0, blocking collectives: 209 us -> none  [per_device(): lax.all_to_all(part_sums, 'ch', split_axis=0, concat_axis=3, tiled=True)]
    dot_general x2 -> x8, matrix products: 85.8 us -> 199 us  [the longest x4 165 us: per_device(): jnp.einsum('ack,kn->anc', field, basis, preferred_element_type=jnp.float32)]
    reshape x0 -> x16, local copies, waits for them, and re-layouts: none -> 102 us  [the longest x4 42.8 us: per_device(): got = got.reshape(width, lat_count * lat_rows, 4 * ch_count * chan_dev)]
    transpose x0 -> x4, local copies, waits for them, and re-layouts: none -> 72.9 us  [per_device(): got = got.transpose(3, 0, 2, 4, 1, 5)]
    another operation x2 -> x1, local copies, waits for them, and re-layouts: 41.6 us -> 0.01 us  [dft_table(): phase = jnp.tile(jnp.array([0, lon_count // 4], jnp.int32), modes.shape[0])]
    dot_general x1 -> x0, local copies, waits for them, and re-layouts: 36 us -> none  [project(): jnp.einsum('brl,lbn->brn', basis_piece, data_rows, preferred_element_type...]
    another operation x2 -> x1, other arithmetic: 22.3 us -> 0.01 us
  transfers between devices with their start and end apart: 2 -> 4, of which waited for: 1 -> 3; matrix products, arithmetic and copies ran while one was open for 20% -> 52% of each run, Pallas kernels for 0% -> 0%
where the time goes in v1:
time: 641 us; the launch traced here: 631 us
  local copies, waits for them, and re-layouts  244 us (38%)
  matrix products  199 us (31%)
  waiting for transfers between devices  139 us (22%)
  other arithmetic  27.2 us (4%)
  starting transfers between devices  20.7 us (3%)
    dot_general x4, matrix products, per_device(): jnp.einsum('ack,kn->anc', field, basis, preferred_element_type=jnp.float32)  165 us
    all_to_all x4, waiting for transfers between devices, per_device(): lax.all_to_all(fourier, ('lat', 'ch'), split_axis=1, concat_axis=0, tiled...  139 us
    transpose x4, local copies, waits for them, and re-layouts, per_device(): got = got.transpose(3, 0, 2, 4, 1, 5)  72.9 us
    reshape x4, local copies, waits for them, and re-layouts, per_device(): got = got.reshape(width, lat_count * lat_rows, 4 * ch_count * chan_dev)  42.8 us
    dot_general x4, matrix products, per_device(): jnp.einsum('brl,bln->brn', legendre[g * width:(g + 1) * width], got, pref...  34.5 us
    convert_element_type x4, local copies, waits for them, and re-layouts, per_device(): fourier = jnp.where(in_grid, fourier * norm_scale, 0.0).astype(jnp.bfloat16)  34.4 us
    reshape x4, local copies, waits for them, and re-layouts, per_device(): fourier = fourier.reshape(lat_rows, dev_count * width, 4 * chan_dev)  33.2 us
    all_to_all x4, local copies, waits for them, and re-layouts, per_device(): lax.all_to_all(fourier, ('lat', 'ch'), split_axis=1, concat_axis=0, tiled...  32.6 us
  transfers between devices with their start and end apart: 4, of which 3 were waited for; matrix products, arithmetic and copies ran while one was open for 52% of the time, Pallas kernels for 0%

profile of v1, /device:TPU:0, one launch (start us, length us, event | category | flops | bytes accessed | tf_op | source)
XLA Modules:
  0.0 631.1 jit_solution(3836355545497258501)
XLA Ops:
  1.8 41.2 %fusion.8 = bf16[91,384,64]{1,0,2:T(8,128)(2,1)} fusion(pred[91]{0:T(512)(128)(4,1)S(1)} %add_compare_fusion, bf16[91,64,1440]{2,1,0:T(8,128)(2,1)} %param.7, s32[384]{0:T(512)S(1)} %add.79, s32[384]{0:T(512)S(1)} %mul.134), kind=kOutput, calls=%fused_computation.13 | convolution fusion | flops 6453669888 | bytes 21249116 | tf_op jit(solution)/shard_map/ack,kn->anc/dot_general | solution.py:45
  42.9 8.6 %copy.44 = bf16[91,384,64]{0,2,1:T(8,128)(2,1)} copy(bf16[91,384,64]{1,0,2:T(8,128)(2,1)} %fusion.8) | data formatting | bytes 8945664 | tf_op jit(solution)/shard_map/convert_element_type | solution.py:46
  68.1 41.2 %fusion.9 = bf16[91,384,64]{1,0,2:T(8,128)(2,1)} fusion(pred[91]{0:T(512)(128)(4,1)S(1)} %add_compare_fusion, bf16[91,64,1440]{2,1,0:T(8,128)(2,1)} %param.7, s32[384]{0:T(512)S(1)} %mul.142, s32[384]{0:T(512)S(1)} %add.79), kind=kOutput, calls=%fused_computation.14 | convolution fusion | flops 6453669888 | bytes 21249116 | tf_op jit(solution)/shard_map/ack,kn->anc/dot_general | solution.py:45
  109.3 8.6 %copy.51 = bf16[91,384,64]{0,2,1:T(8,128)(2,1)} copy(bf16[91,384,64]{1,0,2:T(8,128)(2,1)} %fusion.9) | data formatting | bytes 8945664 | tf_op jit(solution)/shard_map/convert_element_type | solution.py:46
  117.9 8.3 %copy.52 = bf16[91,96,256]{2,0,1:T(8,128)(2,1)} copy(bf16[91,96,256]{0,2,1:T(8,128)(2,1)} %bitcast.81) | data formatting | bytes 8945664 | tf_op jit(solution)/shard_map/reshape | solution.py:47
  126.2 46.4 %all-to-all-done = bf16[91,96,256]{2,0,1:T(8,128)(2,1)} async-done(((bf16[91,96,256]{2,0,1:T(8,128)(2,1)}), bf16[91,96,256]{2,0,1:T(8,128)(2,1)}, u32[]{:S(2)}, u32[]{:S(2)}) %all-to-all-start) | async-done | bytes 4472864 | tf_op jit(solution)/shard_map/all_to_all | solution.py:48
  177.7 41.3 %fusion.10 = bf16[91,384,64]{1,0,2:T(8,128)(2,1)} fusion(pred[91]{0:T(512)(128)(4,1)S(1)} %add_compare_fusion, bf16[91,64,1440]{2,1,0:T(8,128)(2,1)} %param.7, s32[384]{0:T(512)S(1)} %mul.150, s32[384]{0:T(512)S(1)} %add.79), kind=kOutput, calls=%fused_computation.15 | convolution fusion | flops 6453669888 | bytes 21249116 | tf_op jit(solution)/shard_map/ack,kn->anc/dot_general | solution.py:45
  219.0 8.6 %copy.58 = bf16[91,384,64]{0,2,1:T(8,128)(2,1)} copy(bf16[91,384,64]{1,0,2:T(8,128)(2,1)} %fusion.10) | data formatting | bytes 8945664 | tf_op jit(solution)/shard_map/convert_element_type | solution.py:46
  235.9 46.4 %all-to-all-done.1 = bf16[91,96,256]{2,0,1:T(8,128)(2,1)} async-done(((bf16[91,96,256]{2,0,1:T(8,128)(2,1)}), bf16[91,96,256]{2,0,1:T(8,128)(2,1)}, u32[]{:S(2)}, u32[]{:S(2)}) %all-to-all-start.1) | async-done | bytes 4472864 | tf_op jit(solution)/shard_map/all_to_all | solution.py:48
  287.1 41.2 %fusion.11 = bf16[91,384,64]{1,0,2:T(8,128)(2,1)} fusion(pred[91]{0:T(512)(128)(4,1)S(1)} %add_compare_fusion, bf16[91,64,1440]{2,1,0:T(8,128)(2,1)} %param.7, s32[384]{0:T(512)S(1)} %mul.158, s32[384]{0:T(512)S(1)} %add.79), kind=kOutput, calls=%fused_computation.16 | convolution fusion | flops 6453669888 | bytes 21249116 | tf_op jit(solution)/shard_map/ack,kn->anc/dot_general | solution.py:45
  328.3 8.6 %copy.65 = bf16[91,384,64]{0,2,1:T(8,128)(2,1)} copy(bf16[91,384,64]{1,0,2:T(8,128)(2,1)} %fusion.11) | data formatting | bytes 8945664 | tf_op jit(solution)/shard_map/convert_element_type | solution.py:46
  345.2 46.4 %all-to-all-done.2 = bf16[91,96,256]{2,0,1:T(8,128)(2,1)} async-done(((bf16[91,96,256]{2,0,1:T(8,128)(2,1)}), bf16[91,96,256]{2,0,1:T(8,128)(2,1)}, u32[]{:S(2)}, u32[]{:S(2)}) %all-to-all-start.2) | async-done | bytes 4472864 | tf_op jit(solution)/shard_map/all_to_all | solution.py:48
  404.6 18.3 %copy.47 = bf16[3,8,91,4,4,64]{2,1,5,4,3,0:T(8,128)(2,1)} copy(bf16[3,8,91,4,4,64]{2,5,3,0,4,1:T(8,128)(2,1)} %bitcast.76) | data formatting | bytes 8945664 | tf_op jit(solution)/shard_map/transpose | solution.py:50
  422.9 10.7 %reshape.217 = bf16[3,728,1024]{1,2,0:T(8,128)(2,1)} reshape(bf16[3,8,91,4,4,64]{2,1,5,4,3,0:T(8,128)(2,1)} %copy.47) | data formatting | bytes 8945664 | tf_op jit(solution)/shard_map/reshape | solution.py:51
  441.6 18.1 %copy.54 = bf16[3,8,91,4,4,64]{2,1,5,4,3,0:T(8,128)(2,1)} copy(bf16[3,8,91,4,4,64]{2,5,3,0,4,1:T(8,128)(2,1)} %bitcast.77) | data formatting | bytes 8945664 | tf_op jit(solution)/shard_map/transpose | solution.py:50
  459.7 10.7 %reshape.219 = bf16[3,728,1024]{1,2,0:T(8,128)(2,1)} reshape(bf16[3,8,91,4,4,64]{2,1,5,4,3,0:T(8,128)(2,1)} %copy.54) | data formatting | bytes 8945664 | tf_op jit(solution)/shard_map/reshape | solution.py:51
  508.5 18.4 %copy.61 = bf16[3,8,91,4,4,64]{2,1,5,4,3,0:T(8,128)(2,1)} copy(bf16[3,8,91,4,4,64]{2,5,3,0,4,1:T(8,128)(2,1)} %bitcast.78) | data formatting | bytes 8945664 | tf_op jit(solution)/shard_map/transpose | solution.py:50
  526.9 10.7 %reshape.221 = bf16[3,728,1024]{1,2,0:T(8,128)(2,1)} reshape(bf16[3,8,91,4,4,64]{2,1,5,4,3,0:T(8,128)(2,1)} %copy.61) | data formatting | bytes 8945664 | tf_op jit(solution)/shard_map/reshape | solution.py:51
  537.5 10.5 %fusion.30 = f32[3,721,1024]{2,1,0:T(8,128)} fusion(bf16[3,728,1024]{1,2,0:T(8,128)(2,1)} %reshape.221, bf16[12,721,728]{2,1,0:T(8,128)(2,1)} %param.8), kind=kOutput, calls=%fused_computation.35 | convolution fusion | flops 3224911872 | bytes 16932864 | tf_op jit(solution)/shard_map/brl,bln->brn/dot_general | solution.py:52
  556.1 18.1 %copy.68 = bf16[3,8,91,4,4,64]{2,1,5,4,3,0:T(8,128)(2,1)} copy(bf16[3,8,91,4,4,64]{2,5,3,0,4,1:T(8,128)(2,1)} %bitcast.79) | data formatting | bytes 8945664 | tf_op jit(solution)/shard_map/transpose | solution.py:50
  574.3 10.8 %reshape.223 = bf16[3,728,1024]{1,2,0:T(8,128)(2,1)} reshape(bf16[3,8,91,4,4,64]{2,1,5,4,3,0:T(8,128)(2,1)} %copy.68) | data formatting | bytes 8945664 | tf_op jit(solution)/shard_map/reshape | solution.py:51
  585.0 10.8 %fusion.33 = f32[3,721,1024]{2,1,0:T(8,128)} fusion(bf16[3,728,1024]{1,2,0:T(8,128)(2,1)} %reshape.223, bf16[12,721,728]{2,1,0:T(8,128)(2,1)} %param.8), kind=kOutput, calls=%fused_computation.36 | convolution fusion | flops 3224911872 | bytes 16932864 | tf_op jit(solution)/shard_map/brl,bln->brn/dot_general | solution.py:52
  595.8 8.4 %fusion.12 = (f32[3,721,512]{2,1,0:T(8,128)}, f32[3,721,512]{2,1,0:T(8,128)}) fusion(f32[3,721,1024]{2,1,0:T(8,128)} %fusion.33, f32[3]{0:T(128)S(1)} %get-tuple-element.17, pred[3,721]{1,0:T(4,128)(4,1)S(1)} %iota_compare_fusion, f32[3]{0:T(128)S(1)} %get-tuple-element.18, f32[3,721,1024]{2,1,0:T(8,128)S(1)} %bitcast.85, ...), kind=kLoop, calls=%fused_computation.18 | loop fusion | flops 4429824 | bytes 26583294 | tf_op jit(solution)/shard_map/mul | solution.py:60
  617.0 13.8 %pad_maximum_fusion = f32[12,721,2,256]{3,2,1,0:T(2,128)} fusion(f32[3,721,2,256]{3,2,1,0:T(2,128)} %reshape.211, f32[3,721,2,256]{3,2,1,0:T(2,128)} %reshape.206, f32[3,721,2,256]{3,2,1,0:T(2,128)} %reshape.201, f32[3,721,2,256]{3,2,1,0:T(2,128)} %reshape.196), kind=kLoop, calls=%fused_computation | loop fusion | flops 13289472 | bytes 35438592 | tf_op jit(solution)/shard_map/concatenate | solution.py:62
  (63 shorter events, 124.5 us)
Async XLA Ops:
  59.8 112.8 %all-to-all-start = ((bf16[91,96,256]{2,0,1:T(8,128)(2,1)}), bf16[91,96,256]{2,0,1:T(8,128)(2,1)}, u32[]{:S(2)}, u32[]{:S(2)}) async-start(bf16[91,96,256]{2,0,1:T(8,128)(2,1)} %copy.45), calls=%async_computation | async-start | bytes 9437184 | tf_op jit(solution)/shard_map/all_to_all | solution.py:48
  172.6 109.7 %all-to-all-start.1 = ((bf16[91,96,256]{2,0,1:T(8,128)(2,1)}), bf16[91,96,256]{2,0,1:T(8,128)(2,1)}, u32[]{:S(2)}, u32[]{:S(2)}) async-start(bf16[91,96,256]{2,0,1:T(8,128)(2,1)} %copy.52), calls=%async_computation.1 | async-start | bytes 9437184 | tf_op jit(solution)/shard_map/all_to_all | solution.py:48
  282.3 109.3 %all-to-all-start.2 = ((bf16[91,96,256]{2,0,1:T(8,128)(2,1)}), bf16[91,96,256]{2,0,1:T(8,128)(2,1)}, u32[]{:S(2)}, u32[]{:S(2)}) async-start(bf16[91,96,256]{2,0,1:T(8,128)(2,1)} %copy.59), calls=%async_computation.2 | async-start | bytes 9437184 | tf_op jit(solution)/shard_map/all_to_all | solution.py:48
  345.2 50.6 %copy-start = (s32[384]{0:T(512)S(1)}, s32[384]{0:T(512)}, u32[]{:S(2)}) copy-start(s32[384]{0:T(512)} %param.9) | copy-start | bytes 4612
  391.6 156.5 %all-to-all-start.3 = ((bf16[91,96,256]{2,0,1:T(8,128)(2,1)}), bf16[91,96,256]{2,0,1:T(8,128)(2,1)}, u32[]{:S(2)}, u32[]{:S(2)}) async-start(bf16[91,96,256]{2,0,1:T(8,128)(2,1)} %copy.66), calls=%async_computation.3 | async-start | bytes 9437184 | tf_op jit(solution)/shard_map/all_to_all | solution.py:48
  574.3 21.6 %slice-start = ((s8[8945664]{0:T(1024)(128)(4,1)}), s8[557056]{0:T(1024)(128)(4,1)S(1)}, s32[]{:S(2)}) async-start(s8[8945664]{0:T(1024)(128)(4,1)} %bitcast.84), calls=%async_computation.4 | async-start | bytes 1114112
  585.0 10.8 %slice-start.1 = ((s8[8945664]{0:T(1024)(128)(4,1)}), s8[4194304]{0:T(1024)(128)(4,1)S(1)}, s32[]{:S(2)}) async-start(s8[8945664]{0:T(1024)(128)(4,1)} %bitcast.84), calls=%async_computation.5 | async-start | bytes 8388608
  585.0 10.8 %slice-start.2 = ((s8[8945664]{0:T(1024)(128)(4,1)}), s8[4194304]{0:T(1024)(128)(4,1)S(1)}, s32[]{:S(2)}) async-start(s8[8945664]{0:T(1024)(128)(4,1)} %bitcast.84), calls=%async_computation.6 | async-start | bytes 8388608
